TPU v7x, 256 devices: a 2x2x32 block of a 4x8x32 slice. The times are simulated.
256 devices in a mesh: grp: 4 (over y, x), row: 64 (over z, core).
Axes of the slice: x: 2, y: 2, z: 32, core: 2. Of those that a mesh axis runs over, the one named last changes fastest.
The devices are a block of a 4x8x32 slice.
Arguments:
- prior_basis: float32 [262144, 512], P(('grp', 'row')), parts along dimension 0, may hold values from -1 to 1, as said below
- samples: float32 [4, 262144, 64], P(None, ('grp', 'row')), parts along dimension 1, may hold values from -8 to 8
Outputs:
- new_basis: float32 [262144, 256], P(('grp', 'row')), parts along dimension 0
- leaf_estimates: float32 [4, 1024], P(None, ('grp', 'row')), parts along dimension 1
There are 4 independent parts, one for each index of `grp`. A program takes and returns all parts, laid end to end along the dimension named above; each array names one. Nothing has to cross between parts.
Inputs may be any that keep to these rules, and one draw needn't show every extreme that they name: The columns of prior_basis are orthonormal to float32 rounding.
All inputs are finite; a program needn't handle non-finite values.
Results may differ from a plain program's by a relative error of at most 0.0003.
Values sent between devices are 32-bit elements; how exact they have to be, the bound alone decides.
No kernel may reach another device: no remote copies, remote signals or barrier semaphores. Data moves between devices by JAX's collectives and lax.ppermute only.
A program may use at most 64 MiB of HBM per device.

v0:
```python
import functools
import jax
import jax.numpy as jnp
from jax import lax
from jax.sharding import Mesh
from jax.sharding import PartitionSpec as P

LEAF = 256
ROW = ("row_0", "row_1")
GRP_ROW = ("grp", "row_0", "row_1")


def over_axes(array, axes):
    return functools.reduce(lax.psum, axes, array)


def local(prior_basis, samples):
    highest = lax.Precision.HIGHEST
    rounds, local_rows, columns = samples.shape
    total_leaves = local_rows // LEAF * lax.axis_size(ROW)

    def energy_terms(block):
        return jnp.dot(block.T, block, precision=highest)

    prior_terms = jnp.einsum("nk,rns->rks", prior_basis, samples, precision=highest)
    stat_terms = jnp.stack([energy_terms(samples[number]) for number in range(rounds)])
    prior_all, stat_all = lax.psum((prior_terms, stat_terms), ROW)
    new_cols = []
    estimates = []
    for number in range(rounds):
        sample_block = samples[number]
        c_added = None
        if new_cols:
            added = jnp.concatenate(new_cols, axis=1)
        c_prior = prior_all[number]
        stat = stat_all[number]
        if new_cols:
            c_added = over_axes(jnp.dot(added.T, sample_block, precision=highest), ROW)
        remainder = sample_block - jnp.dot(prior_basis, c_prior, precision=highest)
        if new_cols:
            remainder = remainder - jnp.dot(added, c_added, precision=highest)
        gram = stat - jnp.dot(c_prior.T, c_prior, precision=highest)
        if new_cols:
            gram = gram - jnp.dot(c_added.T, c_added, precision=highest)
        energy = jnp.trace(stat)
        factor = jnp.linalg.cholesky(gram)
        fresh_cols = jax.scipy.linalg.solve_triangular(factor, remainder.T, lower=True).T
        leaf_energy = jnp.sum(
            (remainder * remainder).reshape(local_rows // LEAF, LEAF, columns), axis=(1, 2)
        )
        estimates.append(jnp.sqrt(total_leaves * leaf_energy / energy))
        new_cols.append(fresh_cols)
    return (jnp.concatenate(new_cols, axis=1), jnp.stack(estimates))


def solution(mesh):
    split = Mesh(mesh.devices.reshape(mesh.shape["grp"], 32, 2), ("grp", "row_0", "row_1"))
    in_specs = (P(GRP_ROW, None), P(None, GRP_ROW, None))
    out_specs = (P(GRP_ROW, None), P(None, GRP_ROW))
    return jax.shard_map(local, mesh=split, in_specs=in_specs, out_specs=out_specs, check_vma=False)
```

profile of v0, /device:TPU:37, one launch (start us, length us, event | category | flops | bytes accessed | tf_op | source)
XLA Modules:
  0.0 842.6 jit_solution(9579060003339560665)
XLA Ops:
  7.3 1.5 convolution_bitcast_fusion.8
  8.8 1.4 convolution_bitcast_fusion.9
  10.2 1.4 convolution_bitcast_fusion.10
  11.6 1.4 convolution_bitcast_fusion.7
  13.0 4.0 fusion.2
  17.0 0.6 pad_maximum_fusion.7
  17.8 400.5 %all-reduce.3.cloned.1.call-done = (f32[4,512,64]{1,2,0:T(8,128)}, f32[4,64,64]{1,2,0:T(8,128)}) async-done(((f32[4,512,64]{1,2,0:T(8,128)}, f32[4,64,64]{1,2,0:T(8,128)}), (f32[4,512,64]{1,2,0:T(8,128)}, f32[4,64,64]{1,2,0:T(8,128)})) %all-reduce.3.cloned.1.call-update) | async-done | bytes 589840 | tf_op jit(solution)/shard_map/psum | solution.py:27
  418.3 1.6 select_reduce_fusion.7
  419.8 1.2 convolution_subtract_fusion.9
  421.1 1.2 convolution_subtract_fusion.4
  422.3 1.2 convolution_subtract_fusion.6
  423.6 1.8 convolution_subtract_fusion.8
  425.4 3.7 fusion.5
  429.2 2.8 fusion.6
  432.0 2.8 fusion.7
  434.8 2.8 multiply_reduce_fusion.3
  437.7 0.1 copy.25
  437.8 5.8 cholesky.74
  443.6 0.6 compare_reduce_fusion.3
  444.3 0.7 fusion.31
  444.9 4.9 custom-call.8
  449.9 1.6 fusion.14
  451.4 0.4 fusion.20
  451.8 78.4 %psum.58 = f32[64,64]{1,0:T(8,128)S(1)} all-reduce(f32[64,64]{1,0:T(8,128)S(1)} %fusion.20), channel_id=1, replica_groups=mesh['grp'=4,'row_0'=32,'row_1'=2] {'row_0'}, use_global_device_ids=true, to_apply=%region_4.7 | all-reduce | flops 4096 | bytes 32768 | tf_op jit(solution)/shard_map/psum | solution.py:14
  530.2 31.0 %psum.59 = f32[64,64]{1,0:T(8,128)S(1)} all-reduce(f32[64,64]{1,0:T(8,128)S(1)} %psum.58), channel_id=1, replica_groups=mesh['grp'=4,'row_0'=32,'row_1'=2] {'row_1'}, use_global_device_ids=true, to_apply=%region_5.8 | all-reduce | flops 4096 | bytes 32768 | tf_op jit(solution)/shard_map/psum | solution.py:14
  561.2 1.0 convolution_subtract_fusion.7
  562.2 2.1 multiply_reduce_fusion.2
  564.3 0.1 reduce_sum.72
  564.5 0.1 reduce_sum.76
  564.6 0.6 fusion.40
  565.3 6.6 cholesky.85
  571.9 0.6 compare_reduce_fusion.2
  572.5 0.7 fusion.32
  573.2 4.9 custom-call.9
  578.1 1.4 convolution_bitcast_fusion.4
  579.5 0.7 copy-done.2
  580.2 0.7 fusion.10
  580.9 76.9 %psum.60 = f32[128,64]{0,1:T(8,128)S(1)} all-reduce(f32[128,64]{0,1:T(8,128)S(1)} %fusion.10), channel_id=1, replica_groups=mesh['grp'=4,'row_0'=32,'row_1'=2] {'row_0'}, use_global_device_ids=true, to_apply=%region_6.9 | all-reduce | flops 8192 | bytes 65536 | tf_op jit(solution)/shard_map/psum | solution.py:14
  657.8 31.0 %psum.61 = f32[128,64]{0,1:T(8,128)S(1)} all-reduce(f32[128,64]{0,1:T(8,128)S(1)} %psum.60), channel_id=1, replica_groups=mesh['grp'=4,'row_0'=32,'row_1'=2] {'row_1'}, use_global_device_ids=true, to_apply=%region_7.10 | all-reduce | flops 8192 | bytes 65536 | tf_op jit(solution)/shard_map/psum | solution.py:14
  688.8 0.2 convolution_subtract_fusion.5
  689.0 2.2 multiply_reduce_fusion.1
  691.1 0.1 reduce_sum.83
  691.4 5.8 cholesky.96
  697.2 0.6 compare_reduce_fusion.1
  697.9 0.7 fusion.33
  698.5 4.9 custom-call.10
  703.4 1.4 convolution_bitcast_fusion.2
  704.8 0.7 copy-done.3
  705.5 1.8 fusion.9
  707.3 76.7 %psum.62 = f32[192,64]{0,1:T(8,128)S(1)} all-reduce(f32[192,64]{0,1:T(8,128)S(1)} %fusion.9), channel_id=1, replica_groups=mesh['grp'=4,'row_0'=32,'row_1'=2] {'row_0'}, use_global_device_ids=true, to_apply=%region_8.11 | all-reduce | flops 12288 | bytes 98304 | tf_op jit(solution)/shard_map/psum | solution.py:14
  784.0 31.4 %psum.63 = f32[192,64]{0,1:T(8,128)S(1)} all-reduce(f32[192,64]{0,1:T(8,128)S(1)} %psum.62), channel_id=1, replica_groups=mesh['grp'=4,'row_0'=32,'row_1'=2] {'row_1'}, use_global_device_ids=true, to_apply=%region_9.12 | all-reduce | flops 12288 | bytes 98304 | tf_op jit(solution)/shard_map/psum | solution.py:14
  815.4 0.2 convolution_subtract_fusion.3
  815.6 1.7 multiply_reduce_fusion
  817.4 0.1 reduce_sum.106
  817.6 5.8 cholesky.107
  823.5 0.6 compare_reduce_fusion
  824.2 0.7 fusion.34
  824.8 4.9 custom-call.11
  829.7 0.4 convolution_bitcast_fusion
  830.1 1.1 pad_maximum_fusion
  831.3 1.3 copy.35
  832.6 1.3 sqrt_bitcast_fusion.2
  833.9 1.3 sqrt_bitcast_fusion
  835.1 0.6 pad_maximum_fusion.8
  (24 shorter events, 0.5 us)
Async XLA Ops:
  7.2 5.8 copy-start
  7.2 411.1 %all-reduce.3.cloned.1.call-start = ((), (), s32[]{:S(2)}) async-start(), calls=%async_computation | async-start | bytes 1310720 | tf_op jit(solution)/shard_map/psum | solution.py:27
  13.0 412.4 %copy-start.1 = (f32[4,1024,64]{1,2,0:T(8,128)S(1)}, f32[4,1024,64]{1,2,0:T(8,128)}, u32[]{:S(2)}) copy-start(f32[4,1024,64]{1,2,0:T(8,128)} %param.6) | copy-start | bytes 3145732
  418.3 10.9 %copy-start.4 = (f32[4,512,64]{1,2,0:T(8,128)S(1)}, f32[4,512,64]{1,2,0:T(8,128)}, u32[]{:S(2)}) copy-start(f32[4,512,64]{1,2,0:T(8,128)} %get-tuple-element.12) | copy-start | bytes 1572868
  579.5 0.7 copy-start.2
  704.8 0.7 copy-start.3
Sparse Core Ops, SparseCore 0:
  17.9 400.3 all-reduce.2
where the time goes:
time: 843 us
  waiting for transfers between devices  401 us (48%)
  blocking collectives  325 us (39%)
  other arithmetic  56.6 us (7%)
  matrix products  42.5 us (5%)
  between operations  14.4 us (2%)
    psum x1, waiting for transfers between devices, local(): prior_all, stat_all = lax.psum((prior_terms, stat_terms), ROW)  401 us
    psum x6, blocking collectives, over_axes(): return functools.reduce(lax.psum, axes, array)  325 us
    another operation x12, other arithmetic, local(): factor = jnp.linalg.cholesky(gram)  26.8 us
    another operation x8, other arithmetic, local(): jax.scipy.linalg.solve_triangular(factor, remainder.T, lower=True)  22.2 us
  transfers between devices with their start and end apart: 1, of which 1 were waited for; matrix products, arithmetic and copies ran while one was open for 0% of the time, Pallas kernels for 0%

commit v1 on v0

--- a/solution.py
+++ b/solution.py
@@ -24,7 +24,7 @@
 
     prior_terms = jnp.einsum("nk,rns->rks", prior_basis, samples, precision=highest)
     stat_terms = jnp.stack([energy_terms(samples[number]) for number in range(rounds)])
-    prior_all, stat_all = lax.psum((prior_terms, stat_terms), ROW)
+    prior_all, stat_all = lax.psum(lax.psum((prior_terms, stat_terms), "row_1"), "row_0")
     new_cols = []
     estimates = []
     for number in range(rounds):

time: 843 us -> 770 us (0.913)
  waiting for transfers between devices: 401 us -> 306 us
  blocking collectives: 325 us -> 346 us
    psum x1 -> x2, waiting for transfers between devices: 401 us -> 306 us  [the longest x1 240 us: local(): lax.psum(lax.psum((prior_terms, stat_terms), 'row_1'), 'row_0')]
    psum x6, blocking collectives: 325 us -> 346 us  [over_axes(): return functools.reduce(lax.psum, axes, array)]
  transfers between devices with their start and end apart: 1 -> 2, of which waited for: 1 -> 2; matrix products, arithmetic and copies ran while one was open for 0% -> 0% of each run, Pallas kernels for 0% -> 0%
where the time goes in v1:
time: 770 us; the launch traced here: 769 us
  blocking collectives  346 us (45%)
  waiting for transfers between devices  306 us (40%)
  other arithmetic  56.6 us (7%)
  matrix products  42.2 us (5%)
  between operations  14.4 us (2%)
    psum x6, blocking collectives, over_axes(): return functools.reduce(lax.psum, axes, array)  346 us
    psum x1, waiting for transfers between devices, local(): lax.psum(lax.psum((prior_terms, stat_terms), 'row_1'), 'row_0')  240 us
    psum x1, waiting for transfers between devices, local(): lax.psum((prior_terms, stat_terms), 'row_1')  66.4 us
    another operation x12, other arithmetic, local(): factor = jnp.linalg.cholesky(gram)  26.8 us
    another operation x8, other arithmetic, local(): jax.scipy.linalg.solve_triangular(factor, remainder.T, lower=True)  22.2 us
  transfers between devices with their start and end apart: 2, of which 2 were waited for; matrix products, arithmetic and copies ran while one was open for 0% of the time, Pallas kernels for 0%

profile of v1, /device:TPU:37, one launch (start us, length us, event | category | flops | bytes accessed | tf_op | source)
XLA Modules:
  0.0 768.7 jit_solution(11670359480437215078)
XLA Ops:
  7.3 1.5 convolution_bitcast_fusion.8
  8.8 1.4 convolution_bitcast_fusion.9
  10.2 1.4 convolution_bitcast_fusion.10
  11.6 1.4 convolution_bitcast_fusion.7
  13.0 3.9 fusion.2
  16.9 0.7 pad_maximum_fusion.7
  17.7 0.2 all-reduce.5.cloned.1.call-start
  17.9 66.4 %all-reduce.7.cloned.1.call-done = (f32[4,512,64]{1,2,0:T(8,128)}, f32[4,64,64]{1,2,0:T(8,128)}) async-done(((f32[4,512,64]{1,2,0:T(8,128)}, f32[4,64,64]{1,2,0:T(8,128)}), (f32[4,512,64]{1,2,0:T(8,128)}, f32[4,64,64]{1,2,0:T(8,128)})) %all-reduce.7.cloned.1.call-update) | async-done | bytes 589840 | tf_op jit(solution)/shard_map/psum | solution.py:27
  84.3 239.5 %all-reduce.5.cloned.1.call-done = (f32[4,512,64]{1,2,0:T(8,128)}, f32[4,64,64]{1,2,0:T(8,128)}) async-done(((f32[4,512,64]{1,2,0:T(8,128)}, f32[4,64,64]{1,2,0:T(8,128)}), (f32[4,512,64]{1,2,0:T(8,128)}, f32[4,64,64]{1,2,0:T(8,128)})) %all-reduce.5.cloned.1.call-update) | async-done | bytes 589840 | tf_op jit(solution)/shard_map/psum | solution.py:27
  323.9 1.6 select_reduce_fusion.7
  325.4 1.2 convolution_subtract_fusion.9
  326.7 1.2 convolution_subtract_fusion.4
  327.9 1.2 convolution_subtract_fusion.6
  329.2 1.8 convolution_subtract_fusion.8
  331.0 3.7 fusion.5
  334.8 2.8 fusion.6
  337.6 2.8 fusion.7
  340.4 2.8 multiply_reduce_fusion.3
  343.3 5.8 cholesky.74
  349.2 0.6 compare_reduce_fusion.3
  349.9 0.7 fusion.31
  350.5 4.9 custom-call.8
  355.4 1.4 fusion.14
  356.8 0.4 fusion.20
  357.2 78.0 %psum.74 = f32[64,64]{1,0:T(8,128)S(1)} all-reduce(f32[64,64]{1,0:T(8,128)S(1)} %fusion.20), channel_id=1, replica_groups=mesh['grp'=4,'row_0'=32,'row_1'=2] {'row_0'}, use_global_device_ids=true, to_apply=%region_6.9 | all-reduce | flops 4096 | bytes 32768 | tf_op jit(solution)/shard_map/psum | solution.py:14
  435.2 52.3 %psum.75 = f32[64,64]{1,0:T(8,128)S(1)} all-reduce(f32[64,64]{1,0:T(8,128)S(1)} %psum.74), channel_id=1, replica_groups=mesh['grp'=4,'row_0'=32,'row_1'=2] {'row_1'}, use_global_device_ids=true, to_apply=%region_7.10 | all-reduce | flops 4096 | bytes 32768 | tf_op jit(solution)/shard_map/psum | solution.py:14
  487.5 1.0 convolution_subtract_fusion.7
  488.5 2.1 multiply_reduce_fusion.2
  490.6 0.1 reduce_sum.72
  490.9 0.6 fusion.40
  491.5 6.6 cholesky.85
  498.1 0.6 compare_reduce_fusion.2
  498.8 0.7 fusion.32
  499.4 4.9 custom-call.9
  504.3 1.4 convolution_bitcast_fusion.4
  505.7 0.7 copy-done.2
  506.4 0.7 fusion.10
  507.1 76.8 %psum.76 = f32[128,64]{0,1:T(8,128)S(1)} all-reduce(f32[128,64]{0,1:T(8,128)S(1)} %fusion.10), channel_id=1, replica_groups=mesh['grp'=4,'row_0'=32,'row_1'=2] {'row_0'}, use_global_device_ids=true, to_apply=%region_8.11 | all-reduce | flops 8192 | bytes 65536 | tf_op jit(solution)/shard_map/psum | solution.py:14
  583.8 30.7 %psum.77 = f32[128,64]{0,1:T(8,128)S(1)} all-reduce(f32[128,64]{0,1:T(8,128)S(1)} %psum.76), channel_id=1, replica_groups=mesh['grp'=4,'row_0'=32,'row_1'=2] {'row_1'}, use_global_device_ids=true, to_apply=%region_9.12 | all-reduce | flops 8192 | bytes 65536 | tf_op jit(solution)/shard_map/psum | solution.py:14
  614.5 0.2 convolution_subtract_fusion.5
  614.7 2.2 multiply_reduce_fusion.1
  616.9 0.1 reduce_sum.83
  617.1 5.8 cholesky.96
  623.0 0.6 compare_reduce_fusion.1
  623.6 0.7 fusion.33
  624.3 4.9 custom-call.10
  629.2 1.4 convolution_bitcast_fusion.2
  630.6 0.7 copy-done.3
  631.3 1.8 fusion.9
  633.1 78.3 %psum.78 = f32[192,64]{0,1:T(8,128)S(1)} all-reduce(f32[192,64]{0,1:T(8,128)S(1)} %fusion.9), channel_id=1, replica_groups=mesh['grp'=4,'row_0'=32,'row_1'=2] {'row_0'}, use_global_device_ids=true, to_apply=%region_10.13 | all-reduce | flops 12288 | bytes 98304 | tf_op jit(solution)/shard_map/psum | solution.py:14
  711.4 30.1 %psum.79 = f32[192,64]{0,1:T(8,128)S(1)} all-reduce(f32[192,64]{0,1:T(8,128)S(1)} %psum.78), channel_id=1, replica_groups=mesh['grp'=4,'row_0'=32,'row_1'=2] {'row_1'}, use_global_device_ids=true, to_apply=%region_11.14 | all-reduce | flops 12288 | bytes 98304 | tf_op jit(solution)/shard_map/psum | solution.py:14
  741.5 0.2 convolution_subtract_fusion.3
  741.7 1.7 multiply_reduce_fusion
  743.5 0.1 reduce_sum.106
  743.7 5.8 cholesky.107
  749.6 0.6 compare_reduce_fusion
  750.2 0.7 fusion.34
  750.9 4.9 custom-call.11
  755.8 0.4 convolution_bitcast_fusion
  756.2 1.1 pad_maximum_fusion
  757.4 1.3 copy.35
  758.7 1.3 sqrt_bitcast_fusion.2
  759.9 1.3 sqrt_bitcast_fusion
  761.2 0.6 pad_maximum_fusion.8
  (27 shorter events, 0.8 us)
Async XLA Ops:
  7.2 5.8 copy-start
  7.2 77.1 %all-reduce.7.cloned.1.call-start = ((), (), s32[]{:S(2)}) async-start(), calls=%async_computation.1 | async-start | bytes 1310720 | tf_op jit(solution)/shard_map/psum | solution.py:27
  16.9 314.1 %copy-start.1 = (f32[4,1024,64]{1,2,0:T(8,128)S(1)}, f32[4,1024,64]{1,2,0:T(8,128)}, u32[]{:S(2)}) copy-start(f32[4,1024,64]{1,2,0:T(8,128)} %param.6) | copy-start | bytes 3145732
  17.7 306.2 %all-reduce.5.cloned.1.call-start = ((), (), s32[]{:S(2)}) async-start(), calls=%async_computation | async-start | bytes 1310720 | tf_op jit(solution)/shard_map/psum | solution.py:27
  323.9 10.9 %copy-start.4 = (f32[4,512,64]{1,2,0:T(8,128)S(1)}, f32[4,512,64]{1,2,0:T(8,128)}, u32[]{:S(2)}) copy-start(f32[4,512,64]{1,2,0:T(8,128)} %get-tuple-element.12) | copy-start | bytes 1572868
  505.7 0.7 copy-start.2
  630.6 0.7 copy-start.3
Sparse Core Ops, SparseCore 0:
  17.8 66.4 all-reduce.6
  86.7 237.1 all-reduce.4
